TPU v7x, 32 devices: a whole 2x2x4 slice. The times are simulated.
32 devices in a mesh: mem: 4 (over x, core), lat: 8 (over z, y).
Axes of the slice: x: 2, y: 2, z: 4, core: 2. Of those that a mesh axis runs over, the one named last changes fastest.
Arguments:
- control: bfloat16 [8, 10, 704, 1440], P('mem', None, 'lat'), may hold values from -6 to 6
- perturb: bfloat16 [8, 10, 704, 1440], P('mem', None, None, 'lat'), may hold values from -6 to 6
- lon_loc: bfloat16 [1440, 1440], P(None, 'mem'), may hold values from 0 to 1, as said below
- lat_loc: bfloat16 [704, 704], P('mem'), may hold values from 0 to 1, as said below
- static_scale: float32 [10, 704, 1440], P(None, 'mem', 'lat'), may hold values from 0.3 to 1
- static_field: float32 [10, 704, 1440], P(None, 'mem', 'lat'), may hold values from -6 to 6
- courant: float32 [2, 704, 1440], P(None, 'mem', 'lat'), may hold values from -0.48 to 0.48
Outputs:
- increment: float32 [10, 704, 1440], P(None, 'mem', 'lat')
- evolved: float32 [10, 704, 1440], P(None, 'mem', 'lat')
Inputs may be any that keep to these rules, and one draw needn't show every extreme that they name: `lon_loc`: Symmetric, with positive entries. `lat_loc`: Symmetric, with positive entries.
All inputs are finite; a program needn't handle non-finite values.
Results may differ from a plain program's by a relative error of at most 0.0027.
Values may be sent and summed in bfloat16 or wider, within the bound.
No kernel may reach another device: no remote copies, remote signals or barrier semaphores. Data moves between devices by JAX's collectives and lax.ppermute only.
A program may use at most 128 MiB of HBM per device.

v0:
```python
import math
import jax
import jax.numpy as jnp
from jax import lax
from jax.sharding import PartitionSpec as P

NLAT = 704
STEPS = 4


def padded_2(shard, sides, width, wrap):
    for axis, dim in sides:
        size, length = (lax.axis_size(axis), shard.shape[dim])
        up = [(i, (i + 1) % size) for i in range(size if wrap else size - 1)]
        down = [(j, i) for i, j in up]
        last = lax.slice_in_dim(shard, length - width, length, axis=dim)
        leading = lax.slice_in_dim(shard, 0, width, axis=dim)
        before = lax.ppermute(last, axis, up)
        after = lax.ppermute(leading, axis, down)
        shard = jnp.concatenate([before, shard, after], axis=dim)
    return shard


def upwind(padded, east_west, north_south):
    center = padded[:, 1:-1, 1:-1]
    western = padded[:, 1:-1, :-2]
    eastern = padded[:, 1:-1, 2:]
    southern = padded[:, :-2, 1:-1]
    northern = padded[:, 2:, 1:-1]
    zonal = jnp.maximum(east_west, 0.0) * (center - western) + jnp.minimum(east_west, 0.0) * (
        eastern - center
    )
    meridional = jnp.maximum(north_south, 0.0) * (center - southern) + jnp.minimum(
        north_south, 0.0
    ) * (northern - center)
    return center - zonal - meridional


def lon_rim(values, width):
    return padded_2(values, (("lat", 2),), width, True)


def lat_rim(values, width):
    return padded_2(values, (("mem", 1),), width, False)


def evolve(current, courant):
    fields = current.shape[0]
    stacked = jnp.concatenate([current, courant], axis=0)
    extended = lat_rim(lon_rim(stacked, STEPS), STEPS)
    result = extended[:fields]
    wind_ext = extended[fields:]
    for step_index in range(STEPS):
        margin = step_index + 1
        inner_wind = wind_ext[
            :, margin : wind_ext.shape[1] - margin, margin : wind_ext.shape[2] - margin
        ]
        result = upwind(result, inner_wind[0], inner_wind[1])
    return result


def per_device(control, perturb, lon_loc, lat_loc, static_scale, static_field, courant):
    along_lon = jnp.einsum(
        "mfal,lc->amfc",
        control,
        lax.all_gather(lon_loc, "mem", axis=1, tiled=True),
        preferred_element_type=jnp.float32,
    ).astype(jnp.bfloat16)
    banded = lax.all_to_all(along_lon, "lat", split_axis=3, concat_axis=0, tiled=True)
    mem_here = banded.shape[1]
    fields = banded.shape[2]
    lon_width = banded.shape[3]
    flat_band = banded.reshape(banded.shape[0], mem_here * fields * lon_width)
    pert_rows = jnp.transpose(perturb, (2, 0, 1, 3))
    lat_weights_all = lax.all_gather(lat_loc, "mem", axis=0, tiled=True)
    members = mem_here * lax.axis_size("mem")
    ens_scale = 1.0 / math.sqrt(members - 1)
    rows_own = NLAT // lax.axis_size("mem")
    localized = jnp.dot(lat_weights_all, flat_band, preferred_element_type=jnp.float32)
    localized = localized.reshape(NLAT, mem_here, fields, lon_width)
    ensemble_all = jnp.transpose(
        lax.psum(jnp.sum(localized * pert_rows.astype(jnp.float32), axis=1) * ens_scale, "mem"),
        (1, 0, 2),
    )
    offset = lax.axis_index("mem") * rows_own
    ensemble = lax.dynamic_slice_in_dim(ensemble_all, offset, rows_own, 1)
    increment = ensemble + static_scale * static_field
    evolved = evolve(increment, courant)
    return (increment, evolved)


def solution(mesh):
    placed = (
        P("mem", None, "lat", None),
        P("mem", None, None, "lat"),
        P(None, "mem"),
        P("mem", None),
        P(None, "mem", "lat"),
        P(None, "mem", "lat"),
        P(None, "mem", "lat"),
    )
    return jax.shard_map(
        per_device,
        mesh=mesh,
        in_specs=placed,
        out_specs=(P(None, "mem", "lat"), P(None, "mem", "lat")),
        check_vma=False,
    )
```

profile of v0, /device:TPU:1, one launch (start us, length us, event | category | flops | bytes accessed | tf_op | source)
XLA Modules:
  0.0 472.6 jit_solution(8537434043374464706)
XLA Ops:
  7.2 0.0 all-gather.2.cloned.1.call-start
  7.2 2.4 copy.32
  9.6 0.0 all-gather.2.cloned.1.call-update
  9.6 38.8 %all-gather.2.cloned.1.call-done = bf16[1440,1440]{0,1:T(8,128)(2,1)} async-done(((bf16[1440,360]{0,1:T(8,128)(2,1)}), bf16[1440,1440]{0,1:T(8,128)(2,1)}) %all-gather.2.cloned.1.call-update) | async-done | bytes 4147216 | tf_op jit(solution)/shard_map/all_gather | solution.py:66
  48.4 13.5 %convert_bitcast_fusion = bf16[88,2,10,1440]{3,0,2,1:T(8,128)(2,1)} fusion(bf16[2,10,88,1440]{3,2,1,0:T(8,128)(2,1)} %param.7, bf16[1440,1440]{0,1:T(8,128)(2,1)} %all-gather.2.cloned.1.call-done), kind=kOutput, calls=%fused_computation.4 | convolution fusion | flops 7301606400 | bytes 14284800 | tf_op jit(solution)/shard_map/mfal,lc->amfc/dot_general | solution.py:63
  61.8 16.8 %copy.34 = bf16[88,2,10,1440]{0,1,2,3:T(2,128)(2,1)} copy(bf16[88,2,10,1440]{3,0,2,1:T(8,128)(2,1)} %convert_bitcast_fusion) | data formatting | bytes 10137600 | tf_op jit(solution)/shard_map/convert_element_type | solution.py:68
  78.6 5.4 %all-to-all-start = ((bf16[88,2,10,1440]{0,1,2,3:T(2,128)(2,1)}), bf16[88,2,10,1440]{0,1,2,3:T(2,128)(2,1)}, u32[]{:S(2)}, u32[]{:S(2)}) async-start(bf16[88,2,10,1440]{0,1,2,3:T(2,128)(2,1)} %copy.34), calls=%async_computation | async-start | bytes 14745600 | tf_op jit(solution)/shard_map/all_to_all | solution.py:69
  84.0 0.0 all-reduce.2.cloned.1.call-start
  84.0 0.0 copy-done.7
  84.0 10.5 %all_gather.7 = bf16[704,704]{1,0:T(8,128)(2,1)S(1)} all-gather(bf16[176,704]{1,0:T(8,128)(2,1)S(1)} %copy-done.7), channel_id=1, replica_groups=mesh['mem'=4,'lat'=8] {'mem'}, dimensions={0}, use_global_device_ids=true | all-gather | bytes 1239040 | tf_op jit(solution)/shard_map/all_gather | solution.py:75
  94.5 150.4 %all-to-all-done = bf16[88,2,10,1440]{0,1,2,3:T(2,128)(2,1)} async-done(((bf16[88,2,10,1440]{0,1,2,3:T(2,128)(2,1)}), bf16[88,2,10,1440]{0,1,2,3:T(2,128)(2,1)}, u32[]{:S(2)}, u32[]{:S(2)}) %all-to-all-start) | async-done | bytes 5068832 | tf_op jit(solution)/shard_map/all_to_all | solution.py:69
  245.0 8.0 %copy.59 = bf16[88,2,10,8,180]{0,3,4,2,1:T(8,128)(2,1)} copy(bf16[88,2,10,8,180]{0,1,2,4,3:T(2,128)(2,1)} %bitcast.2) | data formatting | bytes 10137600 | tf_op jit(solution)/shard_map/all_to_all | solution.py:69
  253.0 12.2 %reshape.11 = bf16[704,3600]{0,1:T(8,128)(2,1)} reshape(bf16[8,88,2,10,180]{1,0,4,3,2:T(8,128)(2,1)} %bitcast.58) | data formatting | bytes 10137600 | tf_op jit(solution)/shard_map/reshape | solution.py:73
  265.2 9.6 %convolution_bitcast_fusion = f32[704,3600]{1,0:T(8,128)} fusion(bf16[704,3600]{0,1:T(8,128)(2,1)} %reshape.11, bf16[704,704]{1,0:T(8,128)(2,1)S(1)} %all_gather.7), kind=kOutput, calls=%fused_computation.3 | convolution fusion | flops 3568435200 | bytes 16197632 | tf_op jit(solution)/shard_map/dot_general | solution.py:79
  274.7 11.8 %copy.36 = f32[704,3600]{0,1:T(8,128)} copy(f32[704,3600]{1,0:T(8,128)} %convolution_bitcast_fusion) | data formatting | bytes 20275200 | tf_op jit(solution)/shard_map/dot_general | solution.py:79
  286.6 11.6 %reshape.12 = f32[704,2,10,180]{0,3,2,1:T(8,128)} reshape(f32[704,3600]{0,1:T(8,128)} %copy.36) | data formatting | bytes 20275200 | tf_op jit(solution)/shard_map/reshape | solution.py:80
  298.1 10.3 %fusion = f32[704,10,180]{0,2,1:T(8,128)} fusion(f32[704,2,10,180]{0,3,2,1:T(8,128)} %reshape.12, bf16[2,10,704,180]{2,0,3,1:T(2,128)(2,1)} %param.8), kind=kLoop, calls=%fused_computation.1 | loop fusion | flops 6336000 | bytes 20275200 | tf_op jit(solution)/shard_map/reduce_sum | solution.py:82
  308.4 5.5 %broadcast_multiply_fusion = f32[704,10,180]{0,2,1:T(8,128)} fusion(f32[704,10,180]{0,2,1:T(8,128)} %fusion), kind=kLoop, calls=%fused_computation.6 | loop fusion | flops 1267200 | bytes 10137600 | tf_op jit(solution)/shard_map/mul | solution.py:82
  313.9 0.0 all-reduce.2.cloned.1.call-update
  314.0 1.5 copy-done.1
  315.4 1.8 copy.38
  317.3 3.0 copy.39
  320.3 0.0 copy-done.2
  320.3 0.2 copy.40
  320.5 101.5 %all-reduce.2.cloned.1.call-done = f32[704,10,180]{0,2,1:T(8,128)} async-done(((f32[704,10,180]{0,2,1:T(8,128)}), f32[704,10,180]{0,2,1:T(8,128)}) %all-reduce.2.cloned.1.call-update) | async-done | bytes 5068816 | tf_op jit(solution)/shard_map/psum | solution.py:82
  422.0 3.5 bitcast_add_fusion
  425.6 1.2 collective-permute-start
  426.8 3.0 collective-permute-start.1
  429.8 1.6 collective-permute-done
  431.5 0.0 collective-permute-done.1
  431.6 0.3 pad_maximum_fusion
  431.8 1.4 fusion.34
  433.2 2.4 copy.45
  435.6 4.1 collective-permute-start.2
  439.7 1.1 copy.46
  440.8 2.1 collective-permute-start.3
  443.0 1.1 maximum_bitcast_fusion.7
  444.0 0.8 copy.49
  444.8 0.8 copy.50
  445.6 0.8 copy.51
  446.4 0.8 copy.52
  447.2 1.8 copy.53
  449.0 0.0 collective-permute-done.2
  449.0 1.2 copy.47
  450.2 0.0 collective-permute-done.3
  450.3 2.2 copy.48
  452.5 1.3 maximum_bitcast_fusion.3
  453.8 0.0 copy-done
  453.9 0.3 maximum_bitcast_fusion.5
  454.1 0.3 maximum_bitcast_fusion.1
  454.4 1.0 pad_maximum_fusion.1
  455.6 2.1 fusion.4
  457.7 2.0 fusion.28
  459.7 0.0 copy-start.3
  459.7 0.0 copy-start.4
  459.7 0.0 copy-start.5
  459.7 0.0 copy-start.6
  459.8 2.0 fusion.20
  461.8 0.0 copy-done.3
  461.8 0.0 copy-done.4
  461.8 0.0 copy-done.5
  461.8 0.0 copy-done.6
  461.8 2.1 fusion.12
  463.9 1.8 copy.54
  (12 shorter events, 0.2 us)
Async XLA Ops:
  7.2 41.2 %all-gather.2.cloned.1.call-start = ((), (), s32[]{:S(2)}) async-start(), calls=%async_computation.1 | async-start | bytes 5529600 | tf_op jit(solution)/shard_map/all_gather | solution.py:66
  78.6 5.4 %copy-start.7 = (bf16[176,704]{1,0:T(8,128)(2,1)S(1)}, bf16[176,704]{1,0:T(8,128)(2,1)}, u32[]{:S(2)}) copy-start(bf16[176,704]{1,0:T(8,128)(2,1)} %param.10) | copy-start | bytes 743428
  78.6 166.4 %all-to-all-start = ((bf16[88,2,10,1440]{0,1,2,3:T(2,128)(2,1)}), bf16[88,2,10,1440]{0,1,2,3:T(2,128)(2,1)}, u32[]{:S(2)}, u32[]{:S(2)}) async-start(bf16[88,2,10,1440]{0,1,2,3:T(2,128)(2,1)} %copy.34), calls=%async_computation | async-start | bytes 14745600 | tf_op jit(solution)/shard_map/all_to_all | solution.py:69
  84.0 338.0 %all-reduce.2.cloned.1.call-start = ((), (), s32[]{:S(2)}) async-start(), calls=%async_computation.2 | async-start | bytes 11304960 | tf_op jit(solution)/shard_map/psum | solution.py:82
  313.9 1.5 copy-start.1
  317.3 3.0 copy-start.2
  425.6 5.9 %collective-permute-start = (f32[12,176,4]{1,0,2:T(8,128)S(1)}, f32[12,176,4]{1,0,2:T(8,128)S(1)}, u32[]{:S(2)}, u32[]{:S(2)}) collective-permute-start(f32[12,176,4]{1,0,2:T(8,128)S(1)} %copy.41), channel_id=1, source_target_pairs={{0,1},{1,2},{2,3},{3,4},{4,5},{5,6},{6,7},{7,0},{8,9},{9,10},{10,1... | collective-permute-start | bytes 101384 | tf_op jit(solution)/shard_map/ppermute | solution.py:18
  426.8 4.7 collective-permute-start.1
  435.6 13.4 %collective-permute-start.2 = (f32[12,4,188]{2,1,0:T(4,128)}, f32[12,4,188]{2,1,0:T(4,128)}, u32[]{:S(2)}, u32[]{:S(2)}) collective-permute-start(f32[12,4,188]{2,1,0:T(4,128)} %copy.45), channel_id=1, source_target_pairs={{0,8},{8,16},{16,24},{1,9},{9,17},{17,25},{2,10},{10,18},{18,26},{... | collective-permute-start | bytes 108296 | tf_op jit(solution)/shard_map/ppermute | solution.py:18
  440.8 9.4 %collective-permute-start.3 = (f32[12,4,188]{2,1,0:T(4,128)}, f32[12,4,188]{2,1,0:T(4,128)}, u32[]{:S(2)}, u32[]{:S(2)}) collective-permute-start(f32[12,4,188]{2,1,0:T(4,128)} %copy.46), channel_id=1, source_target_pairs={{8,0},{16,8},{24,16},{9,1},{17,9},{25,17},{10,2},{18,10},{26,18},{... | collective-permute-start | bytes 108296 | tf_op jit(solution)/shard_map/ppermute | solution.py:19
  452.5 1.4 copy-start
  459.7 2.1 copy-start.3
  459.7 2.1 copy-start.4
  459.7 2.1 copy-start.5
  459.7 2.1 copy-start.6
Sparse Core Ops, SparseCore 0:
  10.1 38.2 all-gather.1
  314.1 107.8 all-reduce.1
where the time goes:
time: 474 us; the launch traced here: 473 us
  waiting for transfers between devices  292 us (62%)
  local copies, waits for them, and re-layouts  84.6 us (18%)
  other arithmetic  31.8 us (7%)
  matrix products  23 us (5%)
  starting transfers between devices  16 us (3%)
  between operations  14.3 us (3%)
  blocking collectives  10.5 us (2%)
    all_to_all x1, waiting for transfers between devices, per_device(): lax.all_to_all(along_lon, 'lat', split_axis=3, concat_axis=0, tiled=True)  150 us
    psum x1, waiting for transfers between devices, per_device(): lax.psum(jnp.sum(localized * pert_rows.astype(jnp.float32), axis=1) * ens...  102 us
    all_gather x1, waiting for transfers between devices, per_device(): lax.all_gather(lon_loc, 'mem', axis=1, tiled=True)  38.8 us
    convert_element_type x1, local copies, waits for them, and re-layouts, per_device(): along_lon = jnp.einsum('mfal,lc->amfc', control, lax.all_gather(lon_loc,...  16.8 us
    dot_general x1, matrix products, per_device(): jnp.einsum('mfal,lc->amfc', control, lax.all_gather(lon_loc, 'mem', axis=...  13.5 us
    unnamed x22, local copies, waits for them, and re-layouts  12.6 us
    reshape x1, local copies, waits for them, and re-layouts, per_device(): flat_band = banded.reshape(banded.shape[0], mem_here * fields * lon_width)  12.2 us
    dot_general x1, local copies, waits for them, and re-layouts, per_device(): jnp.dot(lat_weights_all, flat_band, preferred_element_type=jnp.float32)  11.8 us
  transfers between devices with their start and end apart: 7, of which 4 were waited for; matrix products, arithmetic and copies ran while one was open for 3% of the time, Pallas kernels for 0%

commit v1 on v0

--- a/solution.py
+++ b/solution.py
@@ -6,6 +6,7 @@
 
 NLAT = 704
 STEPS = 4
+trees_apply = lambda field, along_axis: jnp.sum(lax.all_gather(field, along_axis), 0)
 
 
 def padded_2(shard, sides, width, wrap):
@@ -79,7 +80,9 @@
     localized = jnp.dot(lat_weights_all, flat_band, preferred_element_type=jnp.float32)
     localized = localized.reshape(NLAT, mem_here, fields, lon_width)
     ensemble_all = jnp.transpose(
-        lax.psum(jnp.sum(localized * pert_rows.astype(jnp.float32), axis=1) * ens_scale, "mem"),
+        trees_apply(
+            jnp.sum(localized * pert_rows.astype(jnp.float32), axis=1) * ens_scale, along_axis="mem"
+        ),
         (1, 0, 2),
     )
     offset = lax.axis_index("mem") * rows_own

time: 474 us -> 705 us (1.49)
  waiting for transfers between devices: 292 us -> 465 us
  other arithmetic: 31.8 us -> 82.6 us
    all_gather x0 -> x1, waiting for transfers between devices: none -> 272 us  [lax.all_gather(field, along_axis)]
    psum x1 -> x0, waiting for transfers between devices: 102 us -> none  [per_device(): lax.psum(jnp.sum(localized * pert_rows.astype(jnp.float32), axis=1) * ens...]
    reduce_sum x0 -> x1, other arithmetic: none -> 34.7 us  [jnp.sum(lax.all_gather(field, along_axis), 0)]
    mul x4 -> x1, local copies, waits for them, and re-layouts: 3.15 us -> 12.1 us  [per_device(): jnp.sum(localized * pert_rows.astype(jnp.float32), axis=1) * ens_scale]
  transfers between devices with their start and end apart: 7 -> 7, of which waited for: 4 -> 4; matrix products, arithmetic and copies ran while one was open for 3% -> 1% of each run, Pallas kernels for 0% -> 0%
where the time goes in v1:
time: 705 us; the launch traced here: 699 us
  waiting for transfers between devices  465 us (66%)
  local copies, waits for them, and re-layouts  88.4 us (13%)
  other arithmetic  82.6 us (12%)
  matrix products  23 us (3%)
  starting transfers between devices  15.4 us (2%)
  between operations  14.5 us (2%)
  blocking collectives  10.7 us (2%)
    all_gather x1, waiting for transfers between devices, lax.all_gather(field, along_axis)  272 us
    all_to_all x1, waiting for transfers between devices, per_device(): lax.all_to_all(along_lon, 'lat', split_axis=3, concat_axis=0, tiled=True)  150 us
    all_gather x1, waiting for transfers between devices, per_device(): lax.all_gather(lon_loc, 'mem', axis=1, tiled=True)  38.8 us
    reduce_sum x1, other arithmetic, jnp.sum(lax.all_gather(field, along_axis), 0)  34.7 us
    convert_element_type x1, local copies, waits for them, and re-layouts, per_device(): along_lon = jnp.einsum('mfal,lc->amfc', control, lax.all_gather(lon_loc,...  16.8 us
  transfers between devices with their start and end apart: 7, of which 4 were waited for; matrix products, arithmetic and copies ran while one was open for 1% of the time, Pallas kernels for 0%

profile of v1, /device:TPU:1, one launch (start us, length us, event | category | flops | bytes accessed | tf_op | source)
XLA Modules:
  0.0 699.5 jit_solution(16696181768635476713)
XLA Ops:
  7.2 0.0 all-gather.4.cloned.1.call-start
  7.2 2.4 copy.40
  9.6 0.0 all-gather.4.cloned.1.call-update
  9.6 38.8 %all-gather.4.cloned.1.call-done = bf16[1440,1440]{0,1:T(8,128)(2,1)} async-done(((bf16[1440,360]{0,1:T(8,128)(2,1)}), bf16[1440,1440]{0,1:T(8,128)(2,1)}) %all-gather.4.cloned.1.call-update) | async-done | bytes 4147216 | tf_op jit(solution)/shard_map/all_gather | solution.py:67
  48.4 13.5 %convert_bitcast_fusion = bf16[88,2,10,1440]{3,0,2,1:T(8,128)(2,1)} fusion(bf16[2,10,88,1440]{3,2,1,0:T(8,128)(2,1)} %param.7, bf16[1440,1440]{0,1:T(8,128)(2,1)} %all-gather.4.cloned.1.call-done), kind=kOutput, calls=%fused_computation.4 | convolution fusion | flops 7301606400 | bytes 14284800 | tf_op jit(solution)/shard_map/mfal,lc->amfc/dot_general | solution.py:64
  61.8 16.8 %copy.42 = bf16[88,2,10,1440]{0,1,2,3:T(2,128)(2,1)} copy(bf16[88,2,10,1440]{3,0,2,1:T(8,128)(2,1)} %convert_bitcast_fusion) | data formatting | bytes 10137600 | tf_op jit(solution)/shard_map/convert_element_type | solution.py:69
  78.6 0.0 copy-start.4
  78.6 5.4 all-to-all-start
  84.0 0.0 all-gather.6.cloned.1.call-start
  84.0 0.0 copy-done.4
  84.0 10.7 %all_gather.11 = bf16[704,704]{1,0:T(8,128)(2,1)S(1)} all-gather(bf16[176,704]{1,0:T(8,128)(2,1)S(1)} %copy-done.4), channel_id=1, replica_groups=mesh['mem'=4,'lat'=8] {'mem'}, dimensions={0}, use_global_device_ids=true | all-gather | bytes 1239040 | tf_op jit(solution)/shard_map/all_gather | solution.py:76
  94.7 150.2 %all-to-all-done = bf16[88,2,10,1440]{0,1,2,3:T(2,128)(2,1)} async-done(((bf16[88,2,10,1440]{0,1,2,3:T(2,128)(2,1)}), bf16[88,2,10,1440]{0,1,2,3:T(2,128)(2,1)}, u32[]{:S(2)}, u32[]{:S(2)}) %all-to-all-start) | async-done | bytes 5068832 | tf_op jit(solution)/shard_map/all_to_all | solution.py:70
  245.0 8.0 %copy.88 = bf16[88,2,10,8,180]{0,3,4,2,1:T(8,128)(2,1)} copy(bf16[88,2,10,8,180]{0,1,2,4,3:T(2,128)(2,1)} %bitcast.2) | data formatting | bytes 10137600 | tf_op jit(solution)/shard_map/all_to_all | solution.py:70
  253.0 12.2 %reshape.20 = bf16[704,3600]{0,1:T(8,128)(2,1)} reshape(bf16[8,88,2,10,180]{1,0,4,3,2:T(8,128)(2,1)} %bitcast.66) | data formatting | bytes 10137600 | tf_op jit(solution)/shard_map/reshape | solution.py:74
  265.2 9.5 %convolution_bitcast_fusion = f32[704,3600]{1,0:T(8,128)} fusion(bf16[704,3600]{0,1:T(8,128)(2,1)} %reshape.20, bf16[704,704]{1,0:T(8,128)(2,1)S(1)} %all_gather.11), kind=kOutput, calls=%fused_computation.3 | convolution fusion | flops 3568435200 | bytes 16197632 | tf_op jit(solution)/shard_map/dot_general | solution.py:80
  274.7 11.8 %copy.44 = f32[704,3600]{0,1:T(8,128)} copy(f32[704,3600]{1,0:T(8,128)} %convolution_bitcast_fusion) | data formatting | bytes 20275200 | tf_op jit(solution)/shard_map/dot_general | solution.py:80
  286.6 11.6 %reshape.21 = f32[704,2,10,180]{0,3,2,1:T(8,128)} reshape(f32[704,3600]{0,1:T(8,128)} %copy.44) | data formatting | bytes 20275200 | tf_op jit(solution)/shard_map/reshape | solution.py:81
  298.1 10.3 %fusion = f32[704,10,180]{0,2,1:T(8,128)} fusion(f32[704,2,10,180]{0,3,2,1:T(8,128)} %reshape.21, bf16[2,10,704,180]{2,0,3,1:T(2,128)(2,1)} %param.8), kind=kLoop, calls=%fused_computation.1 | loop fusion | flops 6336000 | bytes 20275200 | tf_op jit(solution)/shard_map/reduce_sum | solution.py:84
  308.4 5.5 broadcast_multiply_fusion
  313.9 12.1 %copy.46 = f32[704,10,180]{2,1,0:T(8,128)} copy(f32[704,10,180]{0,2,1:T(8,128)} %broadcast_multiply_fusion) | data formatting | bytes 10137600 | tf_op jit(solution)/shard_map/mul | solution.py:84
  326.0 0.0 copy-start.2
  326.0 0.0 all-gather.6.cloned.1.call-update
  326.1 1.0 copy-done.2
  327.0 0.3 copy.49
  327.3 271.7 %all-gather.6.cloned.1.call-done = f32[2816,10,180]{2,1,0:T(8,128)} async-done(((f32[704,10,180]{2,1,0:T(8,128)}), f32[2816,10,180]{2,1,0:T(8,128)}) %all-gather.6.cloned.1.call-update) | async-done | bytes 20275216 | tf_op jit(solution)/shard_map/all_gather | solution.py:9
  599.0 34.7 %reduce_sum.19 = f32[704,10,180]{2,1,0:T(8,128)} reduce(f32[4,704,10,180]{3,2,1,0:T(8,128)} %bitcast.65, f32[]{:T(128)} %constant.6.clone.1), dimensions={0}, to_apply=%region_1.0 | reduce | flops 3801600 | bytes 25344004 | tf_op jit(solution)/shard_map/reduce_sum | solution.py:9
  633.7 5.1 bitcast_add_fusion
  638.7 2.2 fusion.34
  641.0 2.0 copy.51
  643.0 4.0 collective-permute-start.1
  647.0 2.0 copy.50
  649.0 0.1 collective-permute-start
  649.0 0.0 collective-permute-done.1
  649.1 1.8 copy.53
  650.8 4.0 collective-permute-done
  654.8 1.8 copy.52
  656.6 0.0 copy-start.3
  656.6 1.0 pad_maximum_fusion.11
  657.6 0.0 copy-start
  657.6 0.0 copy-start.1
  657.6 3.9 collective-permute-start.3
  661.5 2.1 collective-permute-start.2
  663.6 0.0 copy-done.3
  663.6 0.1 maximum_bitcast_fusion.1
  663.7 2.3 copy.54
  665.9 0.0 collective-permute-done.3
  666.0 0.0 collective-permute-done.2
  666.0 0.0 copy-done
  666.0 0.0 copy-done.1
  666.0 2.4 broadcast_maximum_fusion.1
  668.4 0.4 broadcast_minimum_fusion
  668.8 2.3 broadcast_maximum_fusion.3
  671.2 0.4 broadcast_minimum_fusion.2
  671.6 2.3 broadcast_maximum_fusion.5
  673.9 0.4 broadcast_minimum_fusion.4
  674.4 1.6 pad_maximum_fusion
  676.0 3.7 fusion.4
  679.7 3.5 fusion.12
  683.3 3.5 fusion.20
  686.8 3.3 fusion.28
  690.1 2.3 copy.55
  (9 shorter events, 0.2 us)
Async XLA Ops:
  7.2 41.2 %all-gather.4.cloned.1.call-start = ((), (), s32[]{:S(2)}) async-start(), calls=%async_computation.1 | async-start | bytes 5529600 | tf_op jit(solution)/shard_map/all_gather | solution.py:67
  78.6 5.4 copy-start.4
  78.6 166.4 %all-to-all-start = ((bf16[88,2,10,1440]{0,1,2,3:T(2,128)(2,1)}), bf16[88,2,10,1440]{0,1,2,3:T(2,128)(2,1)}, u32[]{:S(2)}, u32[]{:S(2)}) async-start(bf16[88,2,10,1440]{0,1,2,3:T(2,128)(2,1)} %copy.42), calls=%async_computation | async-start | bytes 14745600 | tf_op jit(solution)/shard_map/all_to_all | solution.py:70
  84.0 515.1 %all-gather.6.cloned.1.call-start = ((), (), s32[]{:S(2)}) async-start(), calls=%async_computation.2 | async-start | bytes 57671680 | tf_op jit(solution)/shard_map/all_gather | solution.py:9
  326.0 1.0 copy-start.2
  643.0 6.1 collective-permute-start.1
  649.0 5.9 collective-permute-start
  656.6 7.0 copy-start.3
  657.6 8.3 %copy-start = (f32[12,176,4]{2,0,1:T(8,128)S(1)}, f32[12,176,4]{2,0,1:T(8,128)}, u32[]{:S(2)}) copy-start(f32[12,176,4]{2,0,1:T(8,128)} %copy.53) | copy-start | bytes 101380
  657.6 8.3 %copy-start.1 = (f32[12,176,4]{2,0,1:T(8,128)S(1)}, f32[12,176,4]{2,0,1:T(8,128)}, u32[]{:S(2)}) copy-start(f32[12,176,4]{2,0,1:T(8,128)} %copy.52) | copy-start | bytes 101380
  657.6 8.3 %collective-permute-start.3 = (f32[12,4,188]{2,0,1:T(8,128)S(1)}, f32[12,4,188]{2,0,1:T(8,128)S(1)}, u32[]{:S(2)}, u32[]{:S(2)}) collective-permute-start(f32[12,4,188]{2,0,1:T(8,128)S(1)} %get-tuple-element.25), channel_id=1, source_target_pairs={{8,0},{16,8},{24,16},{9,1},{17,9},{25,17},{10,2},{18,10},{26,18},{... | collective-permute-start | bytes 108296 | tf_op jit(solution)/shard_map/ppermute | solution.py:20
  661.5 4.4 collective-permute-start.2
Sparse Core Ops, SparseCore 0:
  10.1 38.2 all-gather.3
  326.2 272.7 all-gather.5
